TPU v7x, 32 devices: a whole 2x2x4 slice. The times are simulated.
32 devices in a mesh: dp: 16 (over z, y, core), tp: 2 (over x).
Axes of the slice: x: 2, y: 2, z: 4, core: 2. Of those that a mesh axis runs over, the one named last changes fastest.
Arguments:
- hidden: bfloat16 [4096, 4096], P(('dp', 'tp')), may hold values from -6 to 6
- query_grad: bfloat16 [4096, 1024], P('dp', 'tp'), may hold values from -1.5 to 1.5
- key_grad: bfloat16 [4096, 256], P('dp', 'tp'), may hold values from -1.5 to 1.5
- value_grad: bfloat16 [4096, 256], P('dp', 'tp'), may hold values from -1.5 to 1.5
- w_query: bfloat16 [4096, 1024], P(None, 'tp'), may hold values from -0.09375 to 0.09375
- w_key: bfloat16 [4096, 256], P(None, 'tp'), may hold values from -0.09375 to 0.09375
- w_value: bfloat16 [4096, 256], P(None, 'tp'), may hold values from -0.09375 to 0.09375
Outputs:
- hidden_grad: bfloat16 [4096, 4096], P(('dp', 'tp'))
- grad_query: float32 [4096, 1024], P('dp', 'tp')
- grad_key: float32 [4096, 256], P('dp', 'tp')
- grad_value: float32 [4096, 256], P('dp', 'tp')
All inputs are finite; a program needn't handle non-finite values.
Results may differ from a plain program's by a relative error of at most 0.014.
Values may be sent and summed in bfloat16 or wider, within the bound.
A program may use at most 256 MiB of HBM per device.

v0:
```python
import jax
import jax.numpy as jnp
from jax import lax
from jax.sharding import PartitionSpec as P


def contract_rows(left, right):
    return lax.dot_general(
        left, right, (((0,), (0,)), ((), ())), preferred_element_type=jnp.float32
    )


def contract_cols(left, right):
    return lax.dot_general(
        left, right, (((1,), (1,)), ((), ())), preferred_element_type=jnp.float32
    )


def local(hidden, query_grad, key_grad, value_grad, w_query, w_key, w_value):
    query_width = w_query.shape[1]
    head_width = w_key.shape[1]
    all_grads = jnp.concatenate((query_grad, key_grad, value_grad), axis=1)
    all_weights = jnp.concatenate((w_query, w_key, w_value), axis=1)
    picked = all_grads
    total = contract_rows(lax.all_gather(hidden, "tp", axis=0, tiled=True), picked)
    picked = all_grads
    summed = lax.psum_scatter(
        contract_cols(picked, all_weights).astype(jnp.bfloat16),
        "tp",
        scatter_dimension=0,
        tiled=True,
    )
    weight_grad = lax.psum_scatter(
        total.astype(jnp.bfloat16), "dp", scatter_dimension=0, tiled=True
    ).astype(jnp.float32)
    grad_query = weight_grad[:, :query_width]
    grad_key = weight_grad[:, query_width : query_width + head_width]
    grad_value = weight_grad[:, query_width + head_width :]
    return (summed, grad_query, grad_key, grad_value)


def solution(mesh):
    placed = (
        P(("dp", "tp"), None),
        P("dp", "tp"),
        P("dp", "tp"),
        P("dp", "tp"),
        P(None, "tp"),
        P(None, "tp"),
        P(None, "tp"),
    )
    return jax.shard_map(
        local,
        mesh=mesh,
        in_specs=placed,
        out_specs=(P(("dp", "tp"), None), P("dp", "tp"), P("dp", "tp"), P("dp", "tp")),
        check_vma=False,
    )
```

profile of v0, /device:TPU:0, one launch (start us, length us, event | category | flops | bytes accessed | tf_op | source)
XLA Modules:
  0.0 177.1 jit_solution(1083192513753690069)
XLA Ops:
  7.2 0.0 all-gather.2.cloned.1.call-start
  7.2 0.7 all-gather.2.cloned.1.call-update
  7.9 0.0 reduce-scatter.5.cloned.1.call-start
  7.9 1.0 constant_dynamic-update-slice_fusion.2
  8.9 0.9 constant_dynamic-update-slice_fusion.1
  9.8 0.9 constant_dynamic-update-slice_fusion
  10.6 0.0 copy-start
  10.7 0.0 copy-start.1
  10.7 34.7 %all-gather.2.cloned.1.call-done = bf16[256,4096]{1,0:T(8,128)(2,1)} async-done(((bf16[128,4096]{1,0:T(8,128)(2,1)}), bf16[256,4096]{1,0:T(8,128)(2,1)}) %all-gather.2.cloned.1.call-update) | async-done | bytes 2097168 | tf_op jit(solution)/shard_map/all_gather | solution.py:25
  45.4 6.1 %fusion.6 = bf16[4096,768]{0,1:T(8,128)(2,1)} fusion(bf16[256,768]{1,0:T(8,128)(2,1)S(1)} %constant_dynamic-update-slice_fusion, bf16[256,4096]{1,0:T(8,128)(2,1)} %all-gather.2.cloned.1.call-done), kind=kOutput, calls=%fused_computation.7 | convolution fusion | flops 1613758464 | bytes 8781824 | tf_op jit(solution)/shard_map/dot_general | solution.py:8
  51.4 0.0 reduce-scatter.5.cloned.1.call-update
  51.5 0.0 reduce-scatter.3.cloned.1.call-start
  51.5 0.0 copy-done
  51.5 0.0 copy-done.1
  51.5 5.4 %fusion.7 = bf16[256,4096]{1,0:T(8,128)(2,1)} fusion(bf16[256,768]{1,0:T(8,128)(2,1)S(1)} %constant_dynamic-update-slice_fusion, bf16[4096,128]{1,0:T(8,128)(2,1)S(1)} %copy-done, bf16[4096,128]{1,0:T(8,128)(2,1)S(1)} %copy-done.1, bf16[4096,512]{1,0:T(8,128)(2,1)} %param.11), kind=kOutput, calls=%fused_computation.8 | convolution fusion | flops 1630535680 | bytes 8781824 | tf_op jit(solution)/shard_map/dot_general | solution.py:14
  56.9 0.0 reduce-scatter.3.cloned.1.call-update
  56.9 79.8 %reduce-scatter.5.cloned.1.call-done = bf16[256,768]{0,1:T(8,128)(2,1)} async-done(((bf16[4096,768]{0,1:T(8,128)(2,1)}), bf16[256,768]{0,1:T(8,128)(2,1)}) %reduce-scatter.5.cloned.1.call-update) | async-done | bytes 393232 | tf_op jit(solution)/shard_map/reduce_scatter | solution.py:33
  136.7 0.9 fusion.11
  137.6 0.8 copy.12
  138.3 0.8 copy.13
  139.1 1.0 slice.12
  140.1 1.0 copy.11
  141.1 29.4 %reduce-scatter.3.cloned.1.call-done = bf16[128,4096]{1,0:T(8,128)(2,1)} async-done(((bf16[256,4096]{1,0:T(8,128)(2,1)}), bf16[128,4096]{1,0:T(8,128)(2,1)}) %reduce-scatter.3.cloned.1.call-update) | async-done | bytes 1048592 | tf_op jit(solution)/shard_map/reduce_scatter | solution.py:27
Async XLA Ops:
  7.2 38.2 %all-gather.2.cloned.1.call-start = ((), (), s32[]{:S(2)}) async-start(), calls=%async_computation.3 | async-start | bytes 3145728 | tf_op jit(solution)/shard_map/all_gather | solution.py:25
  7.9 128.8 %reduce-scatter.5.cloned.1.call-start = ((), (), s32[]{:S(2)}) async-start(), calls=%async_computation.4 | async-start | bytes 6684672 | tf_op jit(solution)/shard_map/reduce_scatter | solution.py:33
  10.6 40.9 %copy-start = (bf16[4096,128]{1,0:T(8,128)(2,1)S(1)}, bf16[4096,128]{1,0:T(8,128)(2,1)}, u32[]{:S(2)}) copy-start(bf16[4096,128]{1,0:T(8,128)(2,1)} %param.13) | copy-start | bytes 3145732
  10.7 40.9 %copy-start.1 = (bf16[4096,128]{1,0:T(8,128)(2,1)S(1)}, bf16[4096,128]{1,0:T(8,128)(2,1)}, u32[]{:S(2)}) copy-start(bf16[4096,128]{1,0:T(8,128)(2,1)} %param.12) | copy-start | bytes 3145732
  51.5 119.1 %reduce-scatter.3.cloned.1.call-start = ((), (), s32[]{:S(2)}) async-start(), calls=%async_computation.2 | async-start | bytes 3145728 | tf_op jit(solution)/shard_map/reduce_scatter | solution.py:27
Sparse Core Ops, SparseCore 0:
  9.5 35.8 all-gather.1
  51.6 85.0 reduce-scatter.4
  139.5 30.9 reduce-scatter.2
where the time goes:
time: 177 us
  waiting for transfers between devices  145 us (82%)
  between operations  13.8 us (8%)
  matrix products  11.4 us (6%)
  local copies, waits for them, and re-layouts  7.08 us (4%)
    reduce_scatter x1, waiting for transfers between devices, local(): lax.psum_scatter(total.astype(jnp.bfloat16), 'dp', scatter_dimension=0, t...  79.8 us
    all_gather x1, waiting for transfers between devices, local(): lax.all_gather(hidden, 'tp', axis=0, tiled=True)  34.7 us
    reduce_scatter x1, waiting for transfers between devices, local(): lax.psum_scatter(contract_cols(picked, all_weights).astype(jnp.bfloat16),...  29.4 us
    dot_general x1, matrix products, contract_rows(): lax.dot_general(left, right, (((0,), (0,)), ((), ())), preferred_element_...  6.08 us
    dot_general x1, matrix products, contract_cols(): lax.dot_general(left, right, (((1,), (1,)), ((), ())), preferred_element_...  5.36 us
    unnamed x9, local copies, waits for them, and re-layouts  4.35 us
  transfers between devices with their start and end apart: 3, of which 3 were waited for; matrix products, arithmetic and copies ran while one was open for 7% of the time, Pallas kernels for 0%

commit v1 on v0

--- a/solution.py
+++ b/solution.py
@@ -1,7 +1,13 @@
+import functools
+
 import jax
 import jax.numpy as jnp
 from jax import lax
+from jax.experimental import pallas as pl
+from jax.experimental.pallas import tpu as pltpu
 from jax.sharding import PartitionSpec as P
+
+MESH = pl.DeviceIdType.MESH
 
 
 def contract_rows(left, right):
@@ -21,11 +27,9 @@
     head_width = w_key.shape[1]
     all_grads = jnp.concatenate((query_grad, key_grad, value_grad), axis=1)
     all_weights = jnp.concatenate((w_query, w_key, w_value), axis=1)
-    picked = all_grads
-    total = contract_rows(lax.all_gather(hidden, "tp", axis=0, tiled=True), picked)
-    picked = all_grads
+    total = contract_rows(lax.all_gather(hidden, "tp", axis=0, tiled=True), all_grads)
     summed = lax.psum_scatter(
-        contract_cols(picked, all_weights).astype(jnp.bfloat16),
+        contract_cols(all_grads, all_weights).astype(jnp.bfloat16),
         "tp",
         scatter_dimension=0,
         tiled=True,
@@ -37,6 +41,242 @@
     grad_key = weight_grad[:, query_width : query_width + head_width]
     grad_value = weight_grad[:, query_width + head_width :]
     return (summed, grad_query, grad_key, grad_value)
+
+
+def kernel(
+    n_z, pieces,
+    hidden, query_grad, key_grad, value_grad, w_query, w_key, w_value,
+    out_hidden, out_query, out_key, out_value,
+    tokens, grads, weights, head_out, head_in, core_out, core_in,
+    y_out, y_in, total, z_out, z_in, result, final,
+    load_sem, tok_send, tok_recv, head_send, head_recv, core_send, core_recv,
+    y_send, y_recv, z_send, z_recv, store_sem,
+):
+    dp = lax.axis_index("dp")
+    tp = lax.axis_index("tp")
+    core = lax.rem(dp, 2)
+    y = lax.rem(dp // 2, 2)
+    z = dp // 4
+    half = hidden.shape[0]
+    q_w = query_grad.shape[1]
+    k_w = key_grad.shape[1]
+    rows = final.shape[0]
+    pair = 2 * rows
+    width = hidden.shape[1] // pieces
+
+    x_peer = (dp, 1 - tp)
+    core_peer = (dp + 1 - 2 * core, tp)
+    y_peer = (dp + 2 - 4 * y, tp)
+    far_first = sorted(range(1, n_z), key=lambda o: -min(o, n_z - o)) + [0]
+    z_of = [lax.rem(z + o, n_z) for o in far_first]
+
+    def z_peer(k):
+        return (z_of[k] * 4 + y * 2 + core, tp)
+
+    mine = pl.ds(pl.multiple_of(tp * half, half), half)
+    theirs = pl.ds(pl.multiple_of((1 - tp) * half, half), half)
+
+    def load(index, source, target):
+        copy = pltpu.make_async_copy(source, target, load_sem.at[index])
+        copy.start()
+        return copy
+
+    loads = [
+        load(0, query_grad, grads.at[:, pl.ds(0, q_w)]),
+        load(1, key_grad, grads.at[:, pl.ds(q_w, k_w)]),
+        load(2, value_grad, grads.at[:, pl.ds(q_w + k_w, k_w)]),
+        load(3, hidden, tokens.at[mine, :]),
+        load(4, w_query, weights.at[:, pl.ds(0, q_w)]),
+        load(5, w_key, weights.at[:, pl.ds(q_w, k_w)]),
+        load(6, w_value, weights.at[:, pl.ds(q_w + k_w, k_w)]),
+    ]
+
+    barrier = pltpu.get_barrier_semaphore()
+    peers = [x_peer, core_peer, y_peer] + [z_peer(k) for k in range(n_z - 1)]
+    for peer in peers:
+        pl.semaphore_signal(barrier, inc=1, device_id=peer, device_id_type=MESH)
+    pl.semaphore_wait(barrier, len(peers))
+
+    def remote(source, target, send, recv, peer):
+        return pltpu.make_async_remote_copy(
+            src_ref=source, dst_ref=target, send_sem=send, recv_sem=recv,
+            device_id=peer, device_id_type=MESH,
+        )
+
+    def pair_of(k):
+        if k < n_z:
+            return z_of[k] * 2 + (1 - y)
+        return z_of[k - n_z] * 2 + y
+
+    n_pairs = 2 * n_z
+    tok_copies = []
+    for k in range(n_pairs):
+        columns = pl.ds(pl.multiple_of(pair_of(k) * pair, pair), pair)
+        copy = remote(
+            hidden.at[:, columns], tokens.at[mine, columns],
+            tok_send.at[k], tok_recv.at[k], x_peer,
+        )
+        copy.start()
+        tok_copies.append(copy)
+
+    for copy in loads:
+        copy.wait()
+
+    def head_piece(j, carry):
+        columns = pl.ds(pl.multiple_of(j * width, width), width)
+        head_out[j] = contract_cols(
+            grads[theirs, :], weights[columns, :]
+        ).astype(head_out.dtype)
+        return carry
+
+    lax.fori_loop(0, pieces, head_piece, 0)
+
+    head_copies = [
+        remote(
+            head_out.at[j], head_in.at[j], head_send.at[j], head_recv.at[j], x_peer
+        )
+        for j in range(pieces)
+    ]
+    core_copies = [
+        remote(
+            core_out.at[k], core_in.at[k], core_send.at[k], core_recv.at[k], core_peer
+        )
+        for k in range(n_pairs)
+    ]
+    y_copies = [
+        remote(y_out.at[k], y_in.at[k], y_send.at[k], y_recv.at[k], y_peer)
+        for k in range(n_z)
+    ]
+    z_copies = [
+        remote(z_out.at[k], z_in.at[k], z_send.at[k], z_recv.at[k], z_peer(k))
+        for k in range(n_z - 1)
+    ]
+
+    def block(k, which):
+        start = pl.multiple_of(pair_of(k) * pair + which * rows, rows)
+        return contract_rows(tokens[:, pl.ds(start, rows)], grads[...])
+
+    def finish(k):
+        core_copies[k].wait_recv()
+        summed = block(k, core) + core_in[k].astype(jnp.float32)
+        if k < n_z:
+            y_out[k] = summed.astype(y_out.dtype)
+            y_copies[k].start()
+        else:
+            total[k - n_z] = summed
+
+    heads_started = 0
+    for k in range(n_pairs):
+        tok_copies[k].wait_recv()
+        core_out[k] = block(k, 1 - core).astype(core_out.dtype)
+        core_copies[k].start()
+        if k >= 1:
+            finish(k - 1)
+        if k >= 1:
+            stop = pieces * k // (n_pairs - 1)
+            for j in range(heads_started, stop):
+                head_copies[j].start()
+            heads_started = stop
+    finish(n_pairs - 1)
+
+    def forward(k):
+        y_copies[k].wait_recv()
+        summed = total[k] + y_in[k].astype(jnp.float32)
+        if k < n_z - 1:
+            z_out[k] = summed.astype(z_out.dtype)
+            z_copies[k].start()
+        else:
+            for s in range(n_z - 1):
+                z_copies[s].wait_recv()
+                summed = summed + z_in[s].astype(jnp.float32)
+            final[...] = summed
+
+    stores = []
+
+    def add_heads(j):
+        head_copies[j].wait_recv()
+        columns = pl.ds(j * width, width)
+        own = contract_cols(grads[mine, :], weights[columns, :])
+        result[:, columns] = (own + head_in[j].astype(jnp.float32)).astype(result.dtype)
+        copy = pltpu.make_async_copy(
+            result.at[:, columns], out_hidden.at[:, columns], store_sem.at[j]
+        )
+        copy.start()
+        stores.append(copy)
+
+    ready = 0
+    for k in range(n_z):
+        forward(k)
+        if k < n_z - 1:
+            stop = (pieces - 2) * k // max(n_z - 2, 1)
+            for j in range(ready, stop):
+                add_heads(j)
+            ready = max(stop, ready)
+    for index, (target, start, size) in enumerate(
+        ((out_query, 0, q_w), (out_key, q_w, k_w), (out_value, q_w + k_w, k_w))
+    ):
+        copy = pltpu.make_async_copy(
+            final.at[:, pl.ds(start, size)], target, store_sem.at[pieces + index]
+        )
+        copy.start()
+        stores.append(copy)
+    for j in range(ready, pieces):
+        add_heads(j)
+    for copy in tok_copies + head_copies + core_copies + y_copies + z_copies:
+        copy.wait_send()
+    for copy in stores:
+        copy.wait()
+
+
+def fused(n_dp, hidden, query_grad, key_grad, value_grad, w_query, w_key, w_value):
+    half, depth = hidden.shape
+    group = query_grad.shape[0]
+    q_w, k_w = w_query.shape[1], w_key.shape[1]
+    wide = q_w + 2 * k_w
+    rows = depth // n_dp
+    n_z = n_dp // 4
+    n_pairs = 2 * n_z
+    pieces = n_pairs
+    width = depth // pieces
+    bf16, f32 = jnp.bfloat16, jnp.float32
+    dma = pltpu.SemaphoreType.DMA
+    return pl.pallas_call(
+        functools.partial(kernel, n_z, pieces),
+        out_shape=(
+            jax.ShapeDtypeStruct((half, depth), bf16),
+            jax.ShapeDtypeStruct((rows, q_w), f32),
+            jax.ShapeDtypeStruct((rows, k_w), f32),
+            jax.ShapeDtypeStruct((rows, k_w), f32),
+        ),
+        in_specs=[pl.BlockSpec(memory_space=pl.ANY)] * 7,
+        out_specs=(pl.BlockSpec(memory_space=pl.ANY),) * 4,
+        scratch_shapes=[
+            pltpu.VMEM((group, depth), bf16),
+            pltpu.VMEM((group, wide), bf16),
+            pltpu.VMEM((depth, wide), bf16),
+            pltpu.VMEM((pieces, half, width), bf16),
+            pltpu.VMEM((pieces, half, width), bf16),
+            pltpu.VMEM((n_pairs, rows, wide), bf16),
+            pltpu.VMEM((n_pairs, rows, wide), bf16),
+            pltpu.VMEM((n_z, rows, wide), bf16),
+            pltpu.VMEM((n_z, rows, wide), bf16),
+            pltpu.VMEM((n_z, rows, wide), f32),
+            pltpu.VMEM((n_z - 1, rows, wide), bf16),
+            pltpu.VMEM((n_z - 1, rows, wide), bf16),
+            pltpu.VMEM((half, depth), bf16),
+            pltpu.VMEM((rows, wide), f32),
+            dma((7,)),
+            dma((n_pairs,)), dma((n_pairs,)),
+            dma((pieces,)), dma((pieces,)),
+            dma((n_pairs,)), dma((n_pairs,)),
+            dma((n_z,)), dma((n_z,)),
+            dma((n_z - 1,)), dma((n_z - 1,)),
+            dma((pieces + 3,)),
+        ],
+        compiler_params=pltpu.CompilerParams(
+            collective_id=0, has_side_effects=True, vmem_limit_bytes=56 * 1024 * 1024
+        ),
+    )(hidden, query_grad, key_grad, value_grad, w_query, w_key, w_value)
 
 
 def solution(mesh):
@@ -49,8 +289,12 @@
         P(None, "tp"),
         P(None, "tp"),
     )
+    n_dp, n_tp = mesh.shape["dp"], mesh.shape["tp"]
+    body = local
+    if n_tp == 2 and n_dp % 4 == 0 and n_dp > 4:
+        body = functools.partial(fused, n_dp)
     return jax.shard_map(
-        local,
+        body,
         mesh=mesh,
         in_specs=placed,
         out_specs=(P(("dp", "tp"), None), P("dp", "tp"), P("dp", "tp"), P("dp", "tp")),

time: 177 us -> 75.9 us (0.43)
  waiting for transfers between devices: 145 us -> 0 us
  Pallas kernels: 0 us -> 67.6 us
  between operations: 13.8 us -> 0.64 us
  matrix products: 11.4 us -> 0 us
    reduce_scatter x2 -> x0, waiting for transfers between devices: 109 us -> none  [the longest x1 79.8 us: local(): lax.psum_scatter(total.astype(jnp.bfloat16), 'dp', scatter_dimension=0, t...]
    pallas_call x0 -> x1, Pallas kernels: none -> 67.6 us  [fused(): pl.pallas_call(functools.partial(kernel, n_z, pieces), out_shape=(jax.Sha...]
    all_gather x1 -> x0, waiting for transfers between devices: 34.7 us -> none  [local(): lax.all_gather(hidden, 'tp', axis=0, tiled=True)]
    dot_general x2 -> x0, matrix products: 11.4 us -> none  [the longest x1 6.08 us: contract_rows(): lax.dot_general(left, right, (((0,), (0,)), ((), ())), preferred_element_...]
    unnamed x9 -> x4, local copies, waits for them, and re-layouts: 4.35 us -> 7.29 us
    slice x2 -> x0, local copies, waits for them, and re-layouts: 1.87 us -> none  [the longest x1 0.98 us: local(): grad_query = weight_grad[:, :query_width]]
  transfers between devices with their start and end apart: 3 -> 0, of which waited for: 3 -> 0; matrix products, arithmetic and copies ran while one was open for 7% -> 0% of each run, Pallas kernels for 0% -> 0%
where the time goes in v1:
time: 75.9 us; the launch traced here: 75.5 us
  Pallas kernels  67.6 us (89%)
  local copies, waits for them, and re-layouts  7.29 us (10%)
    pallas_call x1, Pallas kernels, fused(): pl.pallas_call(functools.partial(kernel, n_z, pieces), out_shape=(jax.Sha...  67.6 us
    unnamed x4, local copies, waits for them, and re-layouts  7.29 us

profile of v1, /device:TPU:0, one launch (start us, length us, event | category | flops | bytes accessed | tf_op | source)
XLA Modules:
  0.0 75.5 jit_solution(11737832893504929812)
XLA Ops:
  0.6 67.6 %shard_map.102 = (bf16[128,4096]{1,0:T(8,128)(2,1)}, f32[256,512]{1,0:T(8,128)}, f32[256,128]{1,0:T(8,128)}, f32[256,128]{1,0:T(8,128)}) custom-call(bf16[128,4096]{1,0:T(8,128)(2,1)} %hidden.1, bf16[256,512]{1,0:T(8,128)(2,1)} %query_grad.1, bf16[256,128]{1,0:T(8,128)(2,1)} %key_grad.1, bf16[256,128]{1,0:T(8,128)(2,1)} %value_grad.1, ...), custom_call_target="tpu_custom_call" | custom-call | tf_op jit(solution)/shard_map/pallas_call | solution.py:243
  68.2 2.3 %copy.15 = bf16[128,4096]{1,0:T(8,128)(2,1)} copy(bf16[128,4096]{1,0:T(8,128)(2,1)} %get-tuple-element.8) | data formatting | bytes 2097152
  70.5 1.9 %copy.16 = f32[256,512]{1,0:T(8,128)} copy(f32[256,512]{1,0:T(8,128)} %get-tuple-element.9) | data formatting | bytes 1048576
  72.4 1.6 %copy.17 = f32[256,128]{1,0:T(8,128)} copy(f32[256,128]{1,0:T(8,128)} %get-tuple-element.10) | data formatting | bytes 262144
  73.9 1.6 %copy.18 = f32[256,128]{1,0:T(8,128)} copy(f32[256,128]{1,0:T(8,128)} %get-tuple-element.11) | data formatting | bytes 262144

commit v2 on v1

--- a/solution.py
+++ b/solution.py
@@ -46,11 +46,11 @@
 def kernel(
     n_z, pieces,
     hidden, query_grad, key_grad, value_grad, w_query, w_key, w_value,
-    out_hidden, out_query, out_key, out_value,
+    result, final,
     tokens, grads, weights, head_out, head_in, core_out, core_in,
-    y_out, y_in, total, z_out, z_in, result, final,
+    y_out, y_in, total, z_out, z_in,
     load_sem, tok_send, tok_recv, head_send, head_recv, core_send, core_recv,
-    y_send, y_recv, z_send, z_recv, store_sem,
+    y_send, y_recv, z_send, z_recv,
 ):
     dp = lax.axis_index("dp")
     tp = lax.axis_index("tp")
@@ -119,17 +119,8 @@
         copy.start()
         tok_copies.append(copy)
 
-    for copy in loads:
+    for copy in loads[:4]:
         copy.wait()
-
-    def head_piece(j, carry):
-        columns = pl.ds(pl.multiple_of(j * width, width), width)
-        head_out[j] = contract_cols(
-            grads[theirs, :], weights[columns, :]
-        ).astype(head_out.dtype)
-        return carry
-
-    lax.fori_loop(0, pieces, head_piece, 0)
 
     head_copies = [
         remote(
@@ -144,87 +135,115 @@
         for k in range(n_pairs)
     ]
     y_copies = [
-        remote(y_out.at[k], y_in.at[k], y_send.at[k], y_recv.at[k], y_peer)
+        [
+            remote(
+                y_out.at[k, h], y_in.at[k, h],
+                y_send.at[k, h], y_recv.at[k, h], y_peer,
+            )
+            for h in range(2)
+        ]
         for k in range(n_z)
     ]
     z_copies = [
-        remote(z_out.at[k], z_in.at[k], z_send.at[k], z_recv.at[k], z_peer(k))
+        [
+            remote(
+                z_out.at[k, h], z_in.at[k, h],
+                z_send.at[k, h], z_recv.at[k, h], z_peer(k),
+            )
+            for h in range(2)
+        ]
         for k in range(n_z - 1)
     ]
-
-    def block(k, which):
-        start = pl.multiple_of(pair_of(k) * pair + which * rows, rows)
-        return contract_rows(tokens[:, pl.ds(start, rows)], grads[...])
+    part = rows // 2
+
+    def block(k, which, first, size):
+        start = pl.multiple_of(pair_of(k) * pair + which * rows + first, part)
+        return contract_rows(tokens[:, pl.ds(start, size)], grads[...])
 
     def finish(k):
-        core_copies[k].wait_recv()
-        summed = block(k, core) + core_in[k].astype(jnp.float32)
-        if k < n_z:
-            y_out[k] = summed.astype(y_out.dtype)
-            y_copies[k].start()
+        for h in range(2):
+            own = block(k, core, h * part, part)
+            if h == 0:
+                core_copies[k].wait_recv()
+            span = pl.ds(h * part, part)
+            summed = own + core_in[k, span].astype(jnp.float32)
+            if k < n_z:
+                y_out[k, h] = summed.astype(y_out.dtype)
+                y_copies[k][h].start()
+            else:
+                total[k - n_z, h] = summed
+
+    def head_piece(j):
+        columns = pl.ds(j * width, width)
+        head_out[j] = contract_cols(
+            grads[theirs, :], weights[columns, :]
+        ).astype(head_out.dtype)
+        head_copies[j].start()
+
+    def forward(k, h):
+        y_copies[k][h].wait_recv()
+        summed = total[k, h] + y_in[k, h].astype(jnp.float32)
+        if k < n_z - 1:
+            z_out[k, h] = summed.astype(z_out.dtype)
+            z_copies[k][h].start()
         else:
-            total[k - n_z] = summed
-
-    heads_started = 0
+            total[k, h] = summed
+
     for k in range(n_pairs):
         tok_copies[k].wait_recv()
-        core_out[k] = block(k, 1 - core).astype(core_out.dtype)
+        core_out[k] = block(k, 1 - core, 0, rows).astype(core_out.dtype)
         core_copies[k].start()
-        if k >= 1:
-            finish(k - 1)
-        if k >= 1:
-            stop = pieces * k // (n_pairs - 1)
-            for j in range(heads_started, stop):
-                head_copies[j].start()
-            heads_started = stop
-    finish(n_pairs - 1)
-
-    def forward(k):
-        y_copies[k].wait_recv()
-        summed = total[k] + y_in[k].astype(jnp.float32)
-        if k < n_z - 1:
-            z_out[k] = summed.astype(z_out.dtype)
-            z_copies[k].start()
-        else:
-            for s in range(n_z - 1):
-                z_copies[s].wait_recv()
-                summed = summed + z_in[s].astype(jnp.float32)
-            final[...] = summed
-
-    stores = []
+        finish(k)
+        if k == 0:
+            for copy in loads[4:]:
+                copy.wait()
+        head_piece(k)
+        if k == n_z:
+            forward(0, 0)
+            forward(0, 1)
+    assert pieces == n_pairs
 
     def add_heads(j):
         head_copies[j].wait_recv()
         columns = pl.ds(j * width, width)
         own = contract_cols(grads[mine, :], weights[columns, :])
         result[:, columns] = (own + head_in[j].astype(jnp.float32)).astype(result.dtype)
-        copy = pltpu.make_async_copy(
-            result.at[:, columns], out_hidden.at[:, columns], store_sem.at[j]
-        )
-        copy.start()
-        stores.append(copy)
 
     ready = 0
-    for k in range(n_z):
-        forward(k)
-        if k < n_z - 1:
-            stop = (pieces - 2) * k // max(n_z - 2, 1)
-            for j in range(ready, stop):
-                add_heads(j)
-            ready = max(stop, ready)
-    for index, (target, start, size) in enumerate(
-        ((out_query, 0, q_w), (out_key, q_w, k_w), (out_value, q_w + k_w, k_w))
-    ):
-        copy = pltpu.make_async_copy(
-            final.at[:, pl.ds(start, size)], target, store_sem.at[pieces + index]
-        )
-        copy.start()
-        stores.append(copy)
+    for k in range(1, n_z):
+        stop = (pieces - 1) * k // n_z
+        for h in range(2):
+            forward(k, h)
+        for j in range(ready, stop):
+            add_heads(j)
+        ready = stop
+    for h in range(2):
+        span = pl.ds(h * part, part)
+        summed = total[n_z - 1, h]
+        for s in range(n_z - 1):
+            z_copies[s][h].wait_recv()
+            summed = summed + z_in[s, h].astype(jnp.float32)
+        final[span, :] = summed
     for j in range(ready, pieces):
         add_heads(j)
-    for copy in tok_copies + head_copies + core_copies + y_copies + z_copies:
+    flat = [copy for pair in y_copies + z_copies for copy in pair]
+    for copy in tok_copies + head_copies + core_copies + flat:
         copy.wait_send()
-    for copy in stores:
+
+
+def place(result, final, out_hidden, out_query, out_key, out_value, sem):
+    q_w, k_w = out_query.shape[1], out_key.shape[1]
+    copies = [
+        pltpu.make_async_copy(result, out_hidden, sem.at[0]),
+        pltpu.make_async_copy(final.at[:, pl.ds(0, q_w)], out_query, sem.at[1]),
+        pltpu.make_async_copy(final.at[:, pl.ds(q_w, k_w)], out_key, sem.at[2]),
+        pltpu.make_async_copy(
+            final.at[:, pl.ds(q_w + k_w, k_w)], out_value, sem.at[3]
+        ),
+    ]
+    for copy in copies:
+        copy.start()
+    for copy in copies:
         copy.wait()
 
 
@@ -240,16 +259,11 @@
     width = depth // pieces
     bf16, f32 = jnp.bfloat16, jnp.float32
     dma = pltpu.SemaphoreType.DMA
-    return pl.pallas_call(
+    held = pl.pallas_call(
         functools.partial(kernel, n_z, pieces),
-        out_shape=(
-            jax.ShapeDtypeStruct((half, depth), bf16),
-            jax.ShapeDtypeStruct((rows, q_w), f32),
-            jax.ShapeDtypeStruct((rows, k_w), f32),
-            jax.ShapeDtypeStruct((rows, k_w), f32),
-        ),
+        out_shape=(pltpu.VMEM((half, depth), bf16), pltpu.VMEM((rows, wide), f32)),
         in_specs=[pl.BlockSpec(memory_space=pl.ANY)] * 7,
-        out_specs=(pl.BlockSpec(memory_space=pl.ANY),) * 4,
+        out_specs=(pl.BlockSpec(memory_space=pltpu.VMEM),) * 2,
         scratch_shapes=[
             pltpu.VMEM((group, depth), bf16),
             pltpu.VMEM((group, wide), bf16),
@@ -258,25 +272,34 @@
             pltpu.VMEM((pieces, half, width), bf16),
             pltpu.VMEM((n_pairs, rows, wide), bf16),
             pltpu.VMEM((n_pairs, rows, wide), bf16),
-            pltpu.VMEM((n_z, rows, wide), bf16),
-            pltpu.VMEM((n_z, rows, wide), bf16),
-            pltpu.VMEM((n_z, rows, wide), f32),
-            pltpu.VMEM((n_z - 1, rows, wide), bf16),
-            pltpu.VMEM((n_z - 1, rows, wide), bf16),
-            pltpu.VMEM((half, depth), bf16),
-            pltpu.VMEM((rows, wide), f32),
+            pltpu.VMEM((n_z, 2, rows // 2, wide), bf16),
+            pltpu.VMEM((n_z, 2, rows // 2, wide), bf16),
+            pltpu.VMEM((n_z, 2, rows // 2, wide), f32),
+            pltpu.VMEM((n_z - 1, 2, rows // 2, wide), bf16),
+            pltpu.VMEM((n_z - 1, 2, rows // 2, wide), bf16),
             dma((7,)),
             dma((n_pairs,)), dma((n_pairs,)),
             dma((pieces,)), dma((pieces,)),
             dma((n_pairs,)), dma((n_pairs,)),
-            dma((n_z,)), dma((n_z,)),
-            dma((n_z - 1,)), dma((n_z - 1,)),
-            dma((pieces + 3,)),
+            dma((n_z, 2)), dma((n_z, 2)),
+            dma((n_z - 1, 2)), dma((n_z - 1, 2)),
         ],
         compiler_params=pltpu.CompilerParams(
             collective_id=0, has_side_effects=True, vmem_limit_bytes=56 * 1024 * 1024
         ),
     )(hidden, query_grad, key_grad, value_grad, w_query, w_key, w_value)
+    return pl.pallas_call(
+        place,
+        out_shape=(
+            jax.ShapeDtypeStruct((half, depth), bf16),
+            jax.ShapeDtypeStruct((rows, q_w), f32),
+            jax.ShapeDtypeStruct((rows, k_w), f32),
+            jax.ShapeDtypeStruct((rows, k_w), f32),
+        ),
+        in_specs=[pl.BlockSpec(memory_space=pltpu.VMEM)] * 2,
+        out_specs=(pl.BlockSpec(memory_space=pl.ANY),) * 4,
+        scratch_shapes=[dma((4,))],
+    )(*[pltpu.with_memory_space_constraint(a, pltpu.VMEM) for a in held])
 
 
 def solution(mesh):

time: 75.9 us -> 64.2 us (0.85)
  local copies, waits for them, and re-layouts: 7.29 us -> 0 us
  Pallas kernels: 67.6 us -> 63.4 us
    unnamed x4 -> x0, local copies, waits for them, and re-layouts: 7.29 us -> none
    pallas_call x1 -> x2, Pallas kernels: 67.6 us -> 63.4 us  [the longest x1 62.1 us: fused(): pl.pallas_call(functools.partial(kernel, n_z, pieces), out_shape=(pltpu.V...]
where the time goes in v2:
time: 64.2 us; the launch traced here: 64 us
  Pallas kernels  63.4 us (99%)
    pallas_call x1, Pallas kernels, fused(): pl.pallas_call(functools.partial(kernel, n_z, pieces), out_shape=(pltpu.V...  62.1 us

profile of v2, /device:TPU:0, one launch (start us, length us, event | category | flops | bytes accessed | tf_op | source)
XLA Modules:
  0.0 64.0 jit_solution(574990531540705130)
XLA Ops:
  0.6 62.1 %shard_map.102 = (bf16[128,4096]{1,0:T(8,128)(2,1)S(1)}, f32[256,768]{1,0:T(8,128)S(1)}) custom-call(bf16[128,4096]{1,0:T(8,128)(2,1)} %hidden.1, bf16[256,512]{1,0:T(8,128)(2,1)} %query_grad.1, bf16[256,128]{1,0:T(8,128)(2,1)} %key_grad.1, bf16[256,128]{1,0:T(8,128)(2,1)} %value_grad.1, bf16[4096,512]{1,0:T(8,128)(2,1)} %w_query.1, ...), custom_call_target="tpu_custom_call" | custom-call | tf_op jit(solution)/shard_map/pallas_call | solution.py:262
  62.8 1.3 %shard_map.103 = (bf16[128,4096]{1,0:T(8,128)(2,1)}, f32[256,512]{1,0:T(8,128)}, f32[256,128]{1,0:T(8,128)}, f32[256,128]{1,0:T(8,128)}) custom-call(bf16[128,4096]{1,0:T(8,128)(2,1)S(1)} %get-tuple-element.6.result, f32[256,768]{1,0:T(8,128)S(1)} %get-tuple-element.7.final), custom_call_target="tpu_custom_call" | custom-call | tf_op jit(solution)/shard_map/pallas_call | solution.py:291

commit v3 on v2

--- a/solution.py
+++ b/solution.py
@@ -104,9 +104,7 @@
         )
 
     def pair_of(k):
-        if k < n_z:
-            return z_of[k] * 2 + (1 - y)
-        return z_of[k - n_z] * 2 + y
+        return z_of[k // 2] * 2 + (1 - y if k % 2 == 0 else y)
 
     n_pairs = 2 * n_z
     tok_copies = []
@@ -167,11 +165,11 @@
                 core_copies[k].wait_recv()
             span = pl.ds(h * part, part)
             summed = own + core_in[k, span].astype(jnp.float32)
-            if k < n_z:
-                y_out[k, h] = summed.astype(y_out.dtype)
-                y_copies[k][h].start()
+            if k % 2 == 0:
+                y_out[k // 2, h] = summed.astype(y_out.dtype)
+                y_copies[k // 2][h].start()
             else:
-                total[k - n_z, h] = summed
+                total[k // 2, h] = summed
 
     def head_piece(j):
         columns = pl.ds(j * width, width)
@@ -189,6 +187,7 @@
         else:
             total[k, h] = summed
 
+    sent = 0
     for k in range(n_pairs):
         tok_copies[k].wait_recv()
         core_out[k] = block(k, 1 - core, 0, rows).astype(core_out.dtype)
@@ -198,9 +197,9 @@
             for copy in loads[4:]:
                 copy.wait()
         head_piece(k)
-        if k == n_z:
-            forward(0, 0)
-            forward(0, 1)
+        if k >= 2 and k % 3 != 0:
+            forward(sent // 2, sent % 2)
+            sent += 1
     assert pieces == n_pairs
 
     def add_heads(j):
@@ -210,10 +209,9 @@
         result[:, columns] = (own + head_in[j].astype(jnp.float32)).astype(result.dtype)
 
     ready = 0
-    for k in range(1, n_z):
-        stop = (pieces - 1) * k // n_z
-        for h in range(2):
-            forward(k, h)
+    for step in range(sent, 2 * n_z):
+        forward(step // 2, step % 2)
+        stop = (pieces - 1) * (step + 1 - sent) // (2 * n_z - sent)
         for j in range(ready, stop):
             add_heads(j)
         ready = stop

time: 64.2 us -> 58.1 us (0.905)
  Pallas kernels: 63.4 us -> 57.3 us
    pallas_call x1, Pallas kernels: 62.1 us -> 56.1 us  [fused(): pl.pallas_call(functools.partial(kernel, n_z, pieces), out_shape=(pltpu.V...]
where the time goes in v3:
time: 58.1 us; the launch traced here: 58 us
  Pallas kernels  57.3 us (99%)
  between operations  0.64 us (1%)
    pallas_call x1, Pallas kernels, fused(): pl.pallas_call(functools.partial(kernel, n_z, pieces), out_shape=(pltpu.V...  56.1 us
    pallas_call x1, Pallas kernels, fused(): pl.pallas_call(place, out_shape=(jax.ShapeDtypeStruct((half, depth), bf16...  1.25 us

profile of v3, /device:TPU:0, one launch (start us, length us, event | category | flops | bytes accessed | tf_op | source)
XLA Modules:
  0.0 58.0 jit_solution(16963086803399175898)
XLA Ops:
  0.6 56.1 %shard_map.102 = (bf16[128,4096]{1,0:T(8,128)(2,1)S(1)}, f32[256,768]{1,0:T(8,128)S(1)}) custom-call(bf16[128,4096]{1,0:T(8,128)(2,1)} %hidden.1, bf16[256,512]{1,0:T(8,128)(2,1)} %query_grad.1, bf16[256,128]{1,0:T(8,128)(2,1)} %key_grad.1, bf16[256,128]{1,0:T(8,128)(2,1)} %value_grad.1, bf16[4096,512]{1,0:T(8,128)(2,1)} %w_query.1, ...), custom_call_target="tpu_custom_call" | custom-call | tf_op jit(solution)/shard_map/pallas_call | solution.py:260
  56.7 1.3 %shard_map.103 = (bf16[128,4096]{1,0:T(8,128)(2,1)}, f32[256,512]{1,0:T(8,128)}, f32[256,128]{1,0:T(8,128)}, f32[256,128]{1,0:T(8,128)}) custom-call(bf16[128,4096]{1,0:T(8,128)(2,1)S(1)} %get-tuple-element.6.result, f32[256,768]{1,0:T(8,128)S(1)} %get-tuple-element.7.final), custom_call_target="tpu_custom_call" | custom-call | tf_op jit(solution)/shard_map/pallas_call | solution.py:289
